TPU v7x, 32 devices: a whole 2x2x4 slice. The times are simulated.
32 devices in a mesh: dp: 8 (over y, x, core), section: 4 (over z).
Axes of the slice: x: 2, y: 2, z: 4, core: 2. Of those that a mesh axis runs over, the one named last changes fastest.
Arguments:
- activations: bfloat16 [4, 512, 2048], P(None, 'dp'), may hold values from -6 to 6
- cotangent: bfloat16 [4, 512, 2048], P(None, 'dp'), may hold values from -6 to 6
- weight: bfloat16 [4, 2048, 2048], P('section', 'dp'), may hold values from -0.125 to 0.125
- norm_gain: float32 [4, 2048], P('section'), may hold values from 0.1 to 1.9
- pair_mask: int32 [4, 512, 2048], P('section'), may hold values from 0 to 5, as said below
- earlier_mask: int32 [4, 512, 2048], P('section', 'dp'), may hold values from 0 to 5, as said below
Outputs:
- weight_grad: float32 [4, 2048, 2048], P('section', 'dp')
- flip_count: int32 [4], P('section')
Inputs may be any that keep to these rules, and one draw needn't show every extreme that they name: `pair_mask`: pair number of each group of four consecutive rows and each column; pairs numbered (0,1), (0,2), (0,3), (1,2), (1,3), (2,3). `earlier_mask`: pair numbers of the previous step, numbered likewise.
All inputs are finite; a program needn't handle non-finite values.
Results may differ from a plain program's by a relative error of at most 0.02.
Values may be sent and summed in bfloat16 or wider, within the bound.
A program may use at most 64 MiB of HBM per device.

v0:
```python
import math

import jax
import jax.numpy as jnp
from jax import lax
from jax.sharding import PartitionSpec as P

epsilon = 1e-06
decay_rate = 4.0
half_root = 0.7071067811865476
density_scale = 0.3989422804014327
first_table = (0, 0, 0, 1, 1, 2)
second_table = (1, 2, 3, 2, 3, 3)


def shifted(block, axis, distance):
    devices = range(lax.axis_size(axis))
    route = [(i - distance, i) for i in devices if i - distance in devices]
    return lax.ppermute(block, axis, route)


def pair_ends(indices):
    leading = jnp.zeros_like(indices)
    trailing = jnp.zeros_like(indices)
    for pair_index in range(6):
        matches = indices == pair_index
        leading = jnp.where(matches, first_table[pair_index], leading)
        trailing = jnp.where(matches, second_table[pair_index], trailing)
    return (leading, trailing)


def kept_positions(indices):
    leading, trailing = pair_ends(indices)
    groups, columns = indices.shape
    positions = lax.broadcasted_iota(jnp.int32, (groups, 4, columns), 1)
    kept_mask = (positions == leading[:, None, :]) | (positions == trailing[:, None, :])
    return kept_mask.reshape(groups * 4, columns)


def section_forward(inputs, masked, gain_row):
    values = inputs.astype(jnp.float32)
    norm_scale = lax.rsqrt(jnp.mean(values * values, axis=-1, keepdims=True) + epsilon)
    normed = (values * norm_scale * gain_row).astype(jnp.bfloat16)
    preact = jnp.dot(normed, masked, preferred_element_type=jnp.float32)
    normal_cdf = 0.5 * (1.0 + lax.erf(preact * half_root))
    outputs = (values + preact * normal_cdf).astype(jnp.bfloat16)
    return (normed, preact, outputs)


def section_backward(inputs, preact, upstream, masked, gain_row):
    values = inputs.astype(jnp.float32)
    norm_scale = lax.rsqrt(jnp.mean(values * values, axis=-1, keepdims=True) + epsilon)
    normal_cdf = 0.5 * (1.0 + lax.erf(preact * half_root))
    normal_pdf = jnp.exp(-0.5 * preact * preact) * density_scale
    upstream_f = upstream.astype(jnp.float32)
    grad_pre = (upstream_f * (normal_cdf + preact * normal_pdf)).astype(jnp.bfloat16)
    grad_normed = lax.dot_general(
        grad_pre, masked, (((1,), (1,)), ((), ())), preferred_element_type=jnp.float32
    )
    scaled_grad = grad_normed * gain_row
    grad_input = norm_scale * scaled_grad - values * norm_scale**3 * jnp.mean(
        scaled_grad * values, axis=-1, keepdims=True
    )
    return (grad_pre, (upstream_f + grad_input).astype(jnp.bfloat16))


def write_slot(buffer, new_value, slot_index, is_live):
    old_value = lax.dynamic_index_in_dim(buffer, slot_index, 0, keepdims=False)
    chosen = jnp.where(is_live, new_value, old_value)
    return lax.dynamic_update_index_in_dim(buffer, chosen, slot_index, 0)


def body(activations, cotangent, weight, norm_gain, pair_mask, earlier_mask):
    section_count = lax.axis_size("section")
    replica_count = lax.axis_size("dp")
    section_index = lax.axis_index("section")
    replica_index = lax.axis_index("dp")
    micro_count, row_count, model_width = activations.shape
    shard_rows = weight.shape[1]
    groups = shard_rows // 4
    own_weight = weight[0]
    gain_row = norm_gain[0]
    own_pairs = lax.dynamic_slice_in_dim(pair_mask[0], replica_index * groups, groups, 0)
    own_kept = kept_positions(own_pairs)
    earlier_kept = kept_positions(earlier_mask[0])
    flip_local = jnp.sum(own_kept != earlier_kept).reshape(1)
    flip_sum = lax.psum(flip_local, "dp")
    masked_shard = jnp.where(own_kept, own_weight, jnp.zeros_like(own_weight))
    masked = lax.all_gather(masked_shard, "dp", axis=0, tiled=True)
    tick_count = micro_count + section_count - 1
    act_zeros = jnp.zeros((micro_count, row_count, model_width), jnp.bfloat16)
    stored = (act_zeros,)

    def forward_tick(tick_index, state_tuple):
        received, buffers = state_tuple
        micro_index = tick_index - section_index
        is_live = (micro_index >= 0) & (micro_index < micro_count)
        slot_index = jnp.clip(micro_index, 0, micro_count - 1)
        fresh_rows = lax.dynamic_index_in_dim(activations, slot_index, 0, keepdims=False)
        current = jnp.where(section_index == 0, fresh_rows, received)
        normed, preact, outputs = section_forward(current, masked, gain_row)
        results = (current, normed, preact)
        buffers = tuple(
            (
                write_slot(buffer, update, slot_index, is_live)
                for buffer, update in zip(buffers, results)
            )
        )
        received = shifted(outputs, "section", 1)
        return (received, buffers)

    start_rows = jnp.zeros((row_count, model_width), jnp.bfloat16)
    received, stored = lax.fori_loop(0, tick_count, forward_tick, (start_rows, stored))

    def backward_tick(tick_index, state_tuple):
        received, grad_buffer, normed_buffer = state_tuple
        micro_index = tick_index - (section_count - 1 - section_index)
        is_live = (micro_index >= 0) & (micro_index < micro_count)
        slot_index = jnp.clip(micro_index, 0, micro_count - 1)
        fresh_rows = lax.dynamic_index_in_dim(cotangent, slot_index, 0, keepdims=False)
        upstream = jnp.where(section_index == section_count - 1, fresh_rows, received)
        inputs = lax.dynamic_index_in_dim(stored[0], slot_index, 0, keepdims=False)
        normed, preact, unused = section_forward(inputs, masked, gain_row)
        normed_buffer = write_slot(normed_buffer, normed, slot_index, is_live)
        grad_pre, grad_input = section_backward(inputs, preact, upstream, masked, gain_row)
        grad_buffer = write_slot(grad_buffer, grad_pre, slot_index, is_live)
        received = shifted(grad_input, "section", -1)
        return (received, grad_buffer, normed_buffer)

    received, grad_buffer, normed_buffer = lax.fori_loop(
        0, tick_count, backward_tick, (start_rows, act_zeros, act_zeros)
    )
    flat_normed = normed_buffer.reshape(micro_count * row_count, model_width)
    flat_grad = grad_buffer.reshape(micro_count * row_count, model_width)
    summed = lax.psum_scatter(
        lax.dot_general(
            flat_normed, flat_grad, (((0,), (0,)), ((), ())), preferred_element_type=jnp.float32
        ).astype(jnp.bfloat16),
        "dp",
        scatter_dimension=0,
        tiled=True,
    ).astype(jnp.float32)
    token_total = micro_count * row_count * replica_count
    dense_part = summed / math.sqrt(token_total)
    decay_part = jnp.where(own_kept, 0.0, own_weight.astype(jnp.float32))
    gradient = dense_part + decay_rate * decay_part
    return (gradient[None], flip_sum)


def solution(mesh):
    placed = (
        P(None, "dp", None),
        P(None, "dp", None),
        P("section", "dp", None),
        P("section", None),
        P("section", None, None),
        P("section", "dp", None),
    )
    return jax.shard_map(
        body,
        mesh=mesh,
        in_specs=placed,
        out_specs=(P("section", "dp", None), P("section")),
        check_vma=False,
    )
```

profile of v0, /device:TPU:0, one launch (start us, length us, event | category | flops | bytes accessed | tf_op | source)
XLA Modules:
  0.0 414.2 jit_solution(3587117926470875641)
XLA Ops:
  16.7 4.5 %bitcast_select_fusion.3 = (bf16[256,2048]{1,0:T(8,128)(2,1)}, pred[256,2048]{1,0:T(8,128)(4,1)}) fusion(bf16[1,256,2048]{2,1,0:T(8,128)(2,1)} %param.12, s32[256,2048]{1,0:T(8,128)} %eq.207, s32[256,2048]{1,0:T(8,128)} %eq.201, s32[256]{0:T(256)S(1)} %iota.38), kind=kLoop, calls=%fused_computation.74 | loop fusion | flops 2097152 | bytes 6816768 | tf_op jit(solution)/shard_map/jit(_where)/select_n | solution.py:88
  21.4 56.9 %all-gather.2.cloned.1.call-done = bf16[2048,2048]{1,0:T(8,128)(2,1)} async-done(((bf16[256,2048]{1,0:T(8,128)(2,1)}), bf16[2048,2048]{1,0:T(8,128)(2,1)}) %all-gather.2.cloned.1.call-update) | async-done | bytes 8388624 | tf_op jit(solution)/shard_map/all_gather | solution.py:89
  78.5 105.1 %while.35 = (s32[]{:T(128)}, bf16[64,2048]{1,0:T(8,128)(2,1)S(1)}, bf16[4,64,2048]{2,1,0:T(8,128)(2,1)S(1)}, pred[]{:T(512)}, s32[]{:T(128)}, /*index=5*/bf16[4,...) while((s32[]{:T(128)}, bf16[64,2048]{1,0:T(8,128)(2,1)S(1)}, ...), condition=%wide.region_2.3_spmd, body=%wide.region_0.0_spmd.sunk | while | flops 538968128 | bytes 12068064 | solution.py:113
  79.8 5.1 %fusion.69 = bf16[64,2048]{1,0:T(8,128)(2,1)S(1)} fusion(bf16[64,2048]{1,0:T(8,128)(2,1)S(1)} %get-tuple-element.543, bf16[2048,2048]{1,0:T(8,128)(2,1)} %get-tuple-element.593, f32[2048]{0:T(1024)S(1)} %bitcast.94, f32[64]{0:T(128)S(1)} %add_rsqrt_fusion.3), kind=kOutput, calls=%fused_computation.6.clone.1 | convolution fusion | flops 538312704 | bytes 8921344 | tf_op jit(solution)/shard_map/while/body/eval_jaxpr/dot_general | solution.py:44
  88.3 5.9 %collective-permute-done = bf16[64,2048]{1,0:T(8,128)(2,1)S(1)} collective-permute-done((bf16[64,2048]{1,0:T(8,128)(2,1)S(1)}, bf16[64,2048]{1,0:T(8,128)(2,1)S(1)}, u32[]{:S(2)}, u32[]{:S(2)}) %collective-permute-start) | collective-permute-done | bytes 262176 | tf_op jit(solution)/shard_map/while/body/eval_jaxpr/ppermute | solution.py:19
  95.5 5.1 %fusion.69 = bf16[64,2048]{1,0:T(8,128)(2,1)S(1)} fusion(bf16[64,2048]{1,0:T(8,128)(2,1)S(1)} %get-tuple-element.543, bf16[2048,2048]{1,0:T(8,128)(2,1)} %get-tuple-element.593, f32[2048]{0:T(1024)S(1)} %bitcast.94, f32[64]{0:T(128)S(1)} %add_rsqrt_fusion.3), kind=kOutput, calls=%fused_computation.6.clone.1 | convolution fusion | flops 538312704 | bytes 8921344 | tf_op jit(solution)/shard_map/while/body/eval_jaxpr/dot_general | solution.py:44
  100.6 4.4 %collective-permute-start = (bf16[64,2048]{1,0:T(8,128)(2,1)S(1)}, bf16[64,2048]{1,0:T(8,128)(2,1)S(1)}, u32[]{:S(2)}, u32[]{:S(2)}) collective-permute-start(bf16[64,2048]{1,0:T(8,128)(2,1)S(1)} %fusion.69), channel_id=1, source_target_pairs={{0,1},{1,2},{2,3},{4,5},{5,6},{6,7},{8,9},{9,10},{10,11},{12,13},{... | collective-permute-start | bytes 786440 | tf_op jit(solution)/shard_map/while/body/eval_jaxpr/ppermute | solution.py:19
  105.0 5.1 %collective-permute-done = bf16[64,2048]{1,0:T(8,128)(2,1)S(1)} collective-permute-done((bf16[64,2048]{1,0:T(8,128)(2,1)S(1)}, bf16[64,2048]{1,0:T(8,128)(2,1)S(1)}, u32[]{:S(2)}, u32[]{:S(2)}) %collective-permute-start) | collective-permute-done | bytes 262176 | tf_op jit(solution)/shard_map/while/body/eval_jaxpr/ppermute | solution.py:19
  111.3 5.1 %fusion.69 = bf16[64,2048]{1,0:T(8,128)(2,1)S(1)} fusion(bf16[64,2048]{1,0:T(8,128)(2,1)S(1)} %get-tuple-element.543, bf16[2048,2048]{1,0:T(8,128)(2,1)} %get-tuple-element.593, f32[2048]{0:T(1024)S(1)} %bitcast.94, f32[64]{0:T(128)S(1)} %add_rsqrt_fusion.3), kind=kOutput, calls=%fused_computation.6.clone.1 | convolution fusion | flops 538312704 | bytes 8921344 | tf_op jit(solution)/shard_map/while/body/eval_jaxpr/dot_general | solution.py:44
  116.4 4.4 %collective-permute-start = (bf16[64,2048]{1,0:T(8,128)(2,1)S(1)}, bf16[64,2048]{1,0:T(8,128)(2,1)S(1)}, u32[]{:S(2)}, u32[]{:S(2)}) collective-permute-start(bf16[64,2048]{1,0:T(8,128)(2,1)S(1)} %fusion.69), channel_id=1, source_target_pairs={{0,1},{1,2},{2,3},{4,5},{5,6},{6,7},{8,9},{9,10},{10,11},{12,13},{... | collective-permute-start | bytes 786440 | tf_op jit(solution)/shard_map/while/body/eval_jaxpr/ppermute | solution.py:19
  120.8 4.2 %collective-permute-done = bf16[64,2048]{1,0:T(8,128)(2,1)S(1)} collective-permute-done((bf16[64,2048]{1,0:T(8,128)(2,1)S(1)}, bf16[64,2048]{1,0:T(8,128)(2,1)S(1)}, u32[]{:S(2)}, u32[]{:S(2)}) %collective-permute-start) | collective-permute-done | bytes 262176 | tf_op jit(solution)/shard_map/while/body/eval_jaxpr/ppermute | solution.py:19
  126.3 5.1 %fusion.69 = bf16[64,2048]{1,0:T(8,128)(2,1)S(1)} fusion(bf16[64,2048]{1,0:T(8,128)(2,1)S(1)} %get-tuple-element.543, bf16[2048,2048]{1,0:T(8,128)(2,1)} %get-tuple-element.593, f32[2048]{0:T(1024)S(1)} %bitcast.94, f32[64]{0:T(128)S(1)} %add_rsqrt_fusion.3), kind=kOutput, calls=%fused_computation.6.clone.1 | convolution fusion | flops 538312704 | bytes 8921344 | tf_op jit(solution)/shard_map/while/body/eval_jaxpr/dot_general | solution.py:44
  131.4 4.4 %collective-permute-start = (bf16[64,2048]{1,0:T(8,128)(2,1)S(1)}, bf16[64,2048]{1,0:T(8,128)(2,1)S(1)}, u32[]{:S(2)}, u32[]{:S(2)}) collective-permute-start(bf16[64,2048]{1,0:T(8,128)(2,1)S(1)} %fusion.69), channel_id=1, source_target_pairs={{0,1},{1,2},{2,3},{4,5},{5,6},{6,7},{8,9},{9,10},{10,11},{12,13},{... | collective-permute-start | bytes 786440 | tf_op jit(solution)/shard_map/while/body/eval_jaxpr/ppermute | solution.py:19
  135.8 3.9 collective-permute-done
  140.9 5.1 %fusion.69 = bf16[64,2048]{1,0:T(8,128)(2,1)S(1)} fusion(bf16[64,2048]{1,0:T(8,128)(2,1)S(1)} %get-tuple-element.543, bf16[2048,2048]{1,0:T(8,128)(2,1)} %get-tuple-element.593, f32[2048]{0:T(1024)S(1)} %bitcast.94, f32[64]{0:T(128)S(1)} %add_rsqrt_fusion.3), kind=kOutput, calls=%fused_computation.6.clone.1 | convolution fusion | flops 538312704 | bytes 8921344 | tf_op jit(solution)/shard_map/while/body/eval_jaxpr/dot_general | solution.py:44
  146.0 4.4 %collective-permute-start = (bf16[64,2048]{1,0:T(8,128)(2,1)S(1)}, bf16[64,2048]{1,0:T(8,128)(2,1)S(1)}, u32[]{:S(2)}, u32[]{:S(2)}) collective-permute-start(bf16[64,2048]{1,0:T(8,128)(2,1)S(1)} %fusion.69), channel_id=1, source_target_pairs={{0,1},{1,2},{2,3},{4,5},{5,6},{6,7},{8,9},{9,10},{10,11},{12,13},{... | collective-permute-start | bytes 786440 | tf_op jit(solution)/shard_map/while/body/eval_jaxpr/ppermute | solution.py:19
  150.4 3.9 collective-permute-done
  155.6 5.1 %fusion.69 = bf16[64,2048]{1,0:T(8,128)(2,1)S(1)} fusion(bf16[64,2048]{1,0:T(8,128)(2,1)S(1)} %get-tuple-element.543, bf16[2048,2048]{1,0:T(8,128)(2,1)} %get-tuple-element.593, f32[2048]{0:T(1024)S(1)} %bitcast.94, f32[64]{0:T(128)S(1)} %add_rsqrt_fusion.3), kind=kOutput, calls=%fused_computation.6.clone.1 | convolution fusion | flops 538312704 | bytes 8921344 | tf_op jit(solution)/shard_map/while/body/eval_jaxpr/dot_general | solution.py:44
  160.6 4.4 %collective-permute-start = (bf16[64,2048]{1,0:T(8,128)(2,1)S(1)}, bf16[64,2048]{1,0:T(8,128)(2,1)S(1)}, u32[]{:S(2)}, u32[]{:S(2)}) collective-permute-start(bf16[64,2048]{1,0:T(8,128)(2,1)S(1)} %fusion.69), channel_id=1, source_target_pairs={{0,1},{1,2},{2,3},{4,5},{5,6},{6,7},{8,9},{9,10},{10,11},{12,13},{... | collective-permute-start | bytes 786440 | tf_op jit(solution)/shard_map/while/body/eval_jaxpr/ppermute | solution.py:19
  165.1 3.9 collective-permute-done
  170.2 5.1 %fusion.69 = bf16[64,2048]{1,0:T(8,128)(2,1)S(1)} fusion(bf16[64,2048]{1,0:T(8,128)(2,1)S(1)} %get-tuple-element.543, bf16[2048,2048]{1,0:T(8,128)(2,1)} %get-tuple-element.593, f32[2048]{0:T(1024)S(1)} %bitcast.94, f32[64]{0:T(128)S(1)} %add_rsqrt_fusion.3), kind=kOutput, calls=%fused_computation.6.clone.1 | convolution fusion | flops 538312704 | bytes 8921344 | tf_op jit(solution)/shard_map/while/body/eval_jaxpr/dot_general | solution.py:44
  175.3 4.4 %collective-permute-start = (bf16[64,2048]{1,0:T(8,128)(2,1)S(1)}, bf16[64,2048]{1,0:T(8,128)(2,1)S(1)}, u32[]{:S(2)}, u32[]{:S(2)}) collective-permute-start(bf16[64,2048]{1,0:T(8,128)(2,1)S(1)} %fusion.69), channel_id=1, source_target_pairs={{0,1},{1,2},{2,3},{4,5},{5,6},{6,7},{8,9},{9,10},{10,11},{12,13},{... | collective-permute-start | bytes 786440 | tf_op jit(solution)/shard_map/while/body/eval_jaxpr/ppermute | solution.py:19
  179.7 3.9 collective-permute-done
  184.8 141.2 %while.36 = (s32[]{:T(128)}, bf16[64,2048]{1,0:T(8,128)(2,1)S(1)}, bf16[4,64,2048]{2,1,0:T(8,128)(2,1)S(1)}, bf16[4,64,2048]{2,1,0:T(8,128)(2,1)}, pred[]{:T(512...) while((s32[]{:T(128)}, bf16[64,2048]{1,0:T(8,128)(2,1)S(1)}, ...), condition=%wide.region_6.7_spmd, body=%wide.region_3.6_spmd.sunk | while | flops 1080033536 | bytes 24409084 | solution.py:130
  185.0 5.2 %bitcast_dynamic-update-slice_fusion.5 = (bf16[4,64,2048]{2,1,0:T(8,128)(2,1)S(1)}, bf16[64,2048]{1,0:T(8,128)(2,1)S(1)}, f32[64,2048]{1,0:T(8,128)S(1)}) fusion(bf16[4,64,2048]{2,1,0:T(8,128)(2,1)S(1)} %get-tuple-element.614, s32[]{:T(128)S(6)} %min.21, bf16[1,64,2048]{2,1,0:T(8,128)(2,1)S(1)} %constant_dynamic-slice_fusion.5, pred[]{:T(512)S(6)} %and.22, ...), kind=kOutput, calls=%fused_computation.43.clone.1 | convolution fusion | flops 539099136 | bytes 10496001 | tf_op jit(solution)/shard_map/while/body/eval_jaxpr/dot_general | solution.py:44
  190.2 6.2 %fusion.73 = (f32[64]{0:T(128)S(1)}, f32[64,2048]{1,0:T(8,128)S(1)}) fusion(bf16[4,64,2048]{2,1,0:T(8,128)(2,1)S(1)} %get-tuple-element.633, s32[]{:T(128)S(6)} %min.21, f32[2048]{0:T(1024)S(1)} %bitcast.96, bf16[2048,2048]{1,0:T(8,128)(2,1)} %get-tuple-element.635, bf16[64,2048]{1,0:T(8,128)(2,1)S(1)} %get-tuple-element.556, ...), kind=kOutput, calls=%fused_computation.32.clone.1 | convolution fusion | flops 538836928 | bytes 9969924 | tf_op jit(solution)/shard_map/while/body/eval_jaxpr/dot_general | solution.py:57
  199.7 5.6 %collective-permute-done.1 = bf16[64,2048]{1,0:T(8,128)(2,1)S(1)} collective-permute-done((bf16[64,2048]{1,0:T(8,128)(2,1)S(1)}, bf16[64,2048]{1,0:T(8,128)(2,1)S(1)}, u32[]{:S(2)}, u32[]{:S(2)}) %collective-permute-start.1) | collective-permute-done | bytes 262176 | tf_op jit(solution)/shard_map/while/body/eval_jaxpr/ppermute | solution.py:19
  205.6 5.2 %bitcast_dynamic-update-slice_fusion.5 = (bf16[4,64,2048]{2,1,0:T(8,128)(2,1)S(1)}, bf16[64,2048]{1,0:T(8,128)(2,1)S(1)}, f32[64,2048]{1,0:T(8,128)S(1)}) fusion(bf16[4,64,2048]{2,1,0:T(8,128)(2,1)S(1)} %get-tuple-element.614, s32[]{:T(128)S(6)} %min.21, bf16[1,64,2048]{2,1,0:T(8,128)(2,1)S(1)} %constant_dynamic-slice_fusion.5, pred[]{:T(512)S(6)} %and.22, ...), kind=kOutput, calls=%fused_computation.43.clone.1 | convolution fusion | flops 539099136 | bytes 10496001 | tf_op jit(solution)/shard_map/while/body/eval_jaxpr/dot_general | solution.py:44
  210.8 6.2 %fusion.73 = (f32[64]{0:T(128)S(1)}, f32[64,2048]{1,0:T(8,128)S(1)}) fusion(bf16[4,64,2048]{2,1,0:T(8,128)(2,1)S(1)} %get-tuple-element.633, s32[]{:T(128)S(6)} %min.21, f32[2048]{0:T(1024)S(1)} %bitcast.96, bf16[2048,2048]{1,0:T(8,128)(2,1)} %get-tuple-element.635, bf16[64,2048]{1,0:T(8,128)(2,1)S(1)} %get-tuple-element.556, ...), kind=kOutput, calls=%fused_computation.32.clone.1 | convolution fusion | flops 538836928 | bytes 9969924 | tf_op jit(solution)/shard_map/while/body/eval_jaxpr/dot_general | solution.py:57
  220.3 5.1 %collective-permute-done.1 = bf16[64,2048]{1,0:T(8,128)(2,1)S(1)} collective-permute-done((bf16[64,2048]{1,0:T(8,128)(2,1)S(1)}, bf16[64,2048]{1,0:T(8,128)(2,1)S(1)}, u32[]{:S(2)}, u32[]{:S(2)}) %collective-permute-start.1) | collective-permute-done | bytes 262176 | tf_op jit(solution)/shard_map/while/body/eval_jaxpr/ppermute | solution.py:19
  225.7 5.2 %bitcast_dynamic-update-slice_fusion.5 = (bf16[4,64,2048]{2,1,0:T(8,128)(2,1)S(1)}, bf16[64,2048]{1,0:T(8,128)(2,1)S(1)}, f32[64,2048]{1,0:T(8,128)S(1)}) fusion(bf16[4,64,2048]{2,1,0:T(8,128)(2,1)S(1)} %get-tuple-element.614, s32[]{:T(128)S(6)} %min.21, bf16[1,64,2048]{2,1,0:T(8,128)(2,1)S(1)} %constant_dynamic-slice_fusion.5, pred[]{:T(512)S(6)} %and.22, ...), kind=kOutput, calls=%fused_computation.43.clone.1 | convolution fusion | flops 539099136 | bytes 10496001 | tf_op jit(solution)/shard_map/while/body/eval_jaxpr/dot_general | solution.py:44
  230.9 6.2 %fusion.73 = (f32[64]{0:T(128)S(1)}, f32[64,2048]{1,0:T(8,128)S(1)}) fusion(bf16[4,64,2048]{2,1,0:T(8,128)(2,1)S(1)} %get-tuple-element.633, s32[]{:T(128)S(6)} %min.21, f32[2048]{0:T(1024)S(1)} %bitcast.96, bf16[2048,2048]{1,0:T(8,128)(2,1)} %get-tuple-element.635, bf16[64,2048]{1,0:T(8,128)(2,1)S(1)} %get-tuple-element.556, ...), kind=kOutput, calls=%fused_computation.32.clone.1 | convolution fusion | flops 538836928 | bytes 9969924 | tf_op jit(solution)/shard_map/while/body/eval_jaxpr/dot_general | solution.py:57
  240.4 5.1 %collective-permute-done.1 = bf16[64,2048]{1,0:T(8,128)(2,1)S(1)} collective-permute-done((bf16[64,2048]{1,0:T(8,128)(2,1)S(1)}, bf16[64,2048]{1,0:T(8,128)(2,1)S(1)}, u32[]{:S(2)}, u32[]{:S(2)}) %collective-permute-start.1) | collective-permute-done | bytes 262176 | tf_op jit(solution)/shard_map/while/body/eval_jaxpr/ppermute | solution.py:19
  245.7 5.2 %bitcast_dynamic-update-slice_fusion.5 = (bf16[4,64,2048]{2,1,0:T(8,128)(2,1)S(1)}, bf16[64,2048]{1,0:T(8,128)(2,1)S(1)}, f32[64,2048]{1,0:T(8,128)S(1)}) fusion(bf16[4,64,2048]{2,1,0:T(8,128)(2,1)S(1)} %get-tuple-element.614, s32[]{:T(128)S(6)} %min.21, bf16[1,64,2048]{2,1,0:T(8,128)(2,1)S(1)} %constant_dynamic-slice_fusion.5, pred[]{:T(512)S(6)} %and.22, ...), kind=kOutput, calls=%fused_computation.43.clone.1 | convolution fusion | flops 539099136 | bytes 10496001 | tf_op jit(solution)/shard_map/while/body/eval_jaxpr/dot_general | solution.py:44
  251.0 6.2 %fusion.73 = (f32[64]{0:T(128)S(1)}, f32[64,2048]{1,0:T(8,128)S(1)}) fusion(bf16[4,64,2048]{2,1,0:T(8,128)(2,1)S(1)} %get-tuple-element.633, s32[]{:T(128)S(6)} %min.21, f32[2048]{0:T(1024)S(1)} %bitcast.96, bf16[2048,2048]{1,0:T(8,128)(2,1)} %get-tuple-element.635, bf16[64,2048]{1,0:T(8,128)(2,1)S(1)} %get-tuple-element.556, ...), kind=kOutput, calls=%fused_computation.32.clone.1 | convolution fusion | flops 538836928 | bytes 9969924 | tf_op jit(solution)/shard_map/while/body/eval_jaxpr/dot_general | solution.py:57
  260.5 5.1 %collective-permute-done.1 = bf16[64,2048]{1,0:T(8,128)(2,1)S(1)} collective-permute-done((bf16[64,2048]{1,0:T(8,128)(2,1)S(1)}, bf16[64,2048]{1,0:T(8,128)(2,1)S(1)}, u32[]{:S(2)}, u32[]{:S(2)}) %collective-permute-start.1) | collective-permute-done | bytes 262176 | tf_op jit(solution)/shard_map/while/body/eval_jaxpr/ppermute | solution.py:19
  265.8 5.2 %bitcast_dynamic-update-slice_fusion.5 = (bf16[4,64,2048]{2,1,0:T(8,128)(2,1)S(1)}, bf16[64,2048]{1,0:T(8,128)(2,1)S(1)}, f32[64,2048]{1,0:T(8,128)S(1)}) fusion(bf16[4,64,2048]{2,1,0:T(8,128)(2,1)S(1)} %get-tuple-element.614, s32[]{:T(128)S(6)} %min.21, bf16[1,64,2048]{2,1,0:T(8,128)(2,1)S(1)} %constant_dynamic-slice_fusion.5, pred[]{:T(512)S(6)} %and.22, ...), kind=kOutput, calls=%fused_computation.43.clone.1 | convolution fusion | flops 539099136 | bytes 10496001 | tf_op jit(solution)/shard_map/while/body/eval_jaxpr/dot_general | solution.py:44
  271.1 6.2 %fusion.73 = (f32[64]{0:T(128)S(1)}, f32[64,2048]{1,0:T(8,128)S(1)}) fusion(bf16[4,64,2048]{2,1,0:T(8,128)(2,1)S(1)} %get-tuple-element.633, s32[]{:T(128)S(6)} %min.21, f32[2048]{0:T(1024)S(1)} %bitcast.96, bf16[2048,2048]{1,0:T(8,128)(2,1)} %get-tuple-element.635, bf16[64,2048]{1,0:T(8,128)(2,1)S(1)} %get-tuple-element.556, ...), kind=kOutput, calls=%fused_computation.32.clone.1 | convolution fusion | flops 538836928 | bytes 9969924 | tf_op jit(solution)/shard_map/while/body/eval_jaxpr/dot_general | solution.py:57
  280.6 5.1 %collective-permute-done.1 = bf16[64,2048]{1,0:T(8,128)(2,1)S(1)} collective-permute-done((bf16[64,2048]{1,0:T(8,128)(2,1)S(1)}, bf16[64,2048]{1,0:T(8,128)(2,1)S(1)}, u32[]{:S(2)}, u32[]{:S(2)}) %collective-permute-start.1) | collective-permute-done | bytes 262176 | tf_op jit(solution)/shard_map/while/body/eval_jaxpr/ppermute | solution.py:19
  285.9 5.2 %bitcast_dynamic-update-slice_fusion.5 = (bf16[4,64,2048]{2,1,0:T(8,128)(2,1)S(1)}, bf16[64,2048]{1,0:T(8,128)(2,1)S(1)}, f32[64,2048]{1,0:T(8,128)S(1)}) fusion(bf16[4,64,2048]{2,1,0:T(8,128)(2,1)S(1)} %get-tuple-element.614, s32[]{:T(128)S(6)} %min.21, bf16[1,64,2048]{2,1,0:T(8,128)(2,1)S(1)} %constant_dynamic-slice_fusion.5, pred[]{:T(512)S(6)} %and.22, ...), kind=kOutput, calls=%fused_computation.43.clone.1 | convolution fusion | flops 539099136 | bytes 10496001 | tf_op jit(solution)/shard_map/while/body/eval_jaxpr/dot_general | solution.py:44
  291.2 6.2 %fusion.73 = (f32[64]{0:T(128)S(1)}, f32[64,2048]{1,0:T(8,128)S(1)}) fusion(bf16[4,64,2048]{2,1,0:T(8,128)(2,1)S(1)} %get-tuple-element.633, s32[]{:T(128)S(6)} %min.21, f32[2048]{0:T(1024)S(1)} %bitcast.96, bf16[2048,2048]{1,0:T(8,128)(2,1)} %get-tuple-element.635, bf16[64,2048]{1,0:T(8,128)(2,1)S(1)} %get-tuple-element.556, ...), kind=kOutput, calls=%fused_computation.32.clone.1 | convolution fusion | flops 538836928 | bytes 9969924 | tf_op jit(solution)/shard_map/while/body/eval_jaxpr/dot_general | solution.py:57
  300.7 5.1 %collective-permute-done.1 = bf16[64,2048]{1,0:T(8,128)(2,1)S(1)} collective-permute-done((bf16[64,2048]{1,0:T(8,128)(2,1)S(1)}, bf16[64,2048]{1,0:T(8,128)(2,1)S(1)}, u32[]{:S(2)}, u32[]{:S(2)}) %collective-permute-start.1) | collective-permute-done | bytes 262176 | tf_op jit(solution)/shard_map/while/body/eval_jaxpr/ppermute | solution.py:19
  306.0 5.2 %bitcast_dynamic-update-slice_fusion.5 = (bf16[4,64,2048]{2,1,0:T(8,128)(2,1)S(1)}, bf16[64,2048]{1,0:T(8,128)(2,1)S(1)}, f32[64,2048]{1,0:T(8,128)S(1)}) fusion(bf16[4,64,2048]{2,1,0:T(8,128)(2,1)S(1)} %get-tuple-element.614, s32[]{:T(128)S(6)} %min.21, bf16[1,64,2048]{2,1,0:T(8,128)(2,1)S(1)} %constant_dynamic-slice_fusion.5, pred[]{:T(512)S(6)} %and.22, ...), kind=kOutput, calls=%fused_computation.43.clone.1 | convolution fusion | flops 539099136 | bytes 10496001 | tf_op jit(solution)/shard_map/while/body/eval_jaxpr/dot_general | solution.py:44
  311.3 6.2 %fusion.73 = (f32[64]{0:T(128)S(1)}, f32[64,2048]{1,0:T(8,128)S(1)}) fusion(bf16[4,64,2048]{2,1,0:T(8,128)(2,1)S(1)} %get-tuple-element.633, s32[]{:T(128)S(6)} %min.21, f32[2048]{0:T(1024)S(1)} %bitcast.96, bf16[2048,2048]{1,0:T(8,128)(2,1)} %get-tuple-element.635, bf16[64,2048]{1,0:T(8,128)(2,1)S(1)} %get-tuple-element.556, ...), kind=kOutput, calls=%fused_computation.32.clone.1 | convolution fusion | flops 538836928 | bytes 9969924 | tf_op jit(solution)/shard_map/while/body/eval_jaxpr/dot_general | solution.py:57
  320.8 5.1 %collective-permute-done.1 = bf16[64,2048]{1,0:T(8,128)(2,1)S(1)} collective-permute-done((bf16[64,2048]{1,0:T(8,128)(2,1)S(1)}, bf16[64,2048]{1,0:T(8,128)(2,1)S(1)}, u32[]{:S(2)}, u32[]{:S(2)}) %collective-permute-start.1) | collective-permute-done | bytes 262176 | tf_op jit(solution)/shard_map/while/body/eval_jaxpr/ppermute | solution.py:19
  325.9 6.8 %bitcast_convert_fusion = bf16[2048,2048]{1,0:T(8,128)(2,1)} fusion(bf16[4,64,2048]{2,1,0:T(8,128)(2,1)} %get-tuple-element.378, bf16[4,64,2048]{2,1,0:T(8,128)(2,1)S(1)} %get-tuple-element.379), kind=kOutput, calls=%fused_computation.63 | convolution fusion | flops 2151677952 | bytes 10485760 | tf_op jit(solution)/shard_map/dot_general | solution.py:136
  336.1 7.7 %psum.7 = s32[1]{0:T(128)} all-reduce(s32[1]{0:T(128)} %bitcast.16), channel_id=1, replica_groups=mesh['dp'=8,'section'=4] {'dp'}, use_global_device_ids=true, to_apply=%region_9.10 | all-reduce | flops 1 | bytes 8 | tf_op jit(solution)/shard_map/psum | solution.py:87
  343.8 60.3 %reduce-scatter.2.cloned.1.call-done = bf16[256,2048]{1,0:T(8,128)(2,1)} async-done(((bf16[2048,2048]{1,0:T(8,128)(2,1)}), bf16[256,2048]{1,0:T(8,128)(2,1)}) %reduce-scatter.2.cloned.1.call-update) | async-done | bytes 1048592 | tf_op jit(solution)/shard_map/reduce_scatter | solution.py:135
  (111 shorter events, 54.4 us)
Async XLA Ops:
  7.2 71.2 %all-gather.2.cloned.1.call-start = ((), (), s32[]{:S(2)}) async-start(), calls=%async_computation.1 | async-start | bytes 9437184 | tf_op jit(solution)/shard_map/all_gather | solution.py:89
  8.7 0.8 copy-start.1
  10.0 1.8 copy-start.6
  21.2 57.3 %copy-start = (f32[1,2048]{1,0:T(1,128)S(1)}, f32[1,2048]{1,0:T(1,128)}, u32[]{:S(2)}) copy-start(f32[1,2048]{1,0:T(1,128)} %param.13) | copy-start | bytes 24580
  21.2 382.9 %reduce-scatter.2.cloned.1.call-start = ((), (), s32[]{:S(2)}) async-start(), calls=%async_computation.2 | async-start | bytes 9437184 | tf_op jit(solution)/shard_map/reduce_scatter | solution.py:135
  84.9 9.4 %collective-permute-start = (bf16[64,2048]{1,0:T(8,128)(2,1)S(1)}, bf16[64,2048]{1,0:T(8,128)(2,1)S(1)}, u32[]{:S(2)}, u32[]{:S(2)}) collective-permute-start(bf16[64,2048]{1,0:T(8,128)(2,1)S(1)} %fusion.69), channel_id=1, source_target_pairs={{0,1},{1,2},{2,3},{4,5},{5,6},{6,7},{8,9},{9,10},{10,11},{12,13},{... | collective-permute-start | bytes 786440 | tf_op jit(solution)/shard_map/while/body/eval_jaxpr/ppermute | solution.py:19
  100.6 9.5 %collective-permute-start = (bf16[64,2048]{1,0:T(8,128)(2,1)S(1)}, bf16[64,2048]{1,0:T(8,128)(2,1)S(1)}, u32[]{:S(2)}, u32[]{:S(2)}) collective-permute-start(bf16[64,2048]{1,0:T(8,128)(2,1)S(1)} %fusion.69), channel_id=1, source_target_pairs={{0,1},{1,2},{2,3},{4,5},{5,6},{6,7},{8,9},{9,10},{10,11},{12,13},{... | collective-permute-start | bytes 786440 | tf_op jit(solution)/shard_map/while/body/eval_jaxpr/ppermute | solution.py:19
  116.4 8.6 %collective-permute-start = (bf16[64,2048]{1,0:T(8,128)(2,1)S(1)}, bf16[64,2048]{1,0:T(8,128)(2,1)S(1)}, u32[]{:S(2)}, u32[]{:S(2)}) collective-permute-start(bf16[64,2048]{1,0:T(8,128)(2,1)S(1)} %fusion.69), channel_id=1, source_target_pairs={{0,1},{1,2},{2,3},{4,5},{5,6},{6,7},{8,9},{9,10},{10,11},{12,13},{... | collective-permute-start | bytes 786440 | tf_op jit(solution)/shard_map/while/body/eval_jaxpr/ppermute | solution.py:19
  131.4 8.3 %collective-permute-start = (bf16[64,2048]{1,0:T(8,128)(2,1)S(1)}, bf16[64,2048]{1,0:T(8,128)(2,1)S(1)}, u32[]{:S(2)}, u32[]{:S(2)}) collective-permute-start(bf16[64,2048]{1,0:T(8,128)(2,1)S(1)} %fusion.69), channel_id=1, source_target_pairs={{0,1},{1,2},{2,3},{4,5},{5,6},{6,7},{8,9},{9,10},{10,11},{12,13},{... | collective-permute-start | bytes 786440 | tf_op jit(solution)/shard_map/while/body/eval_jaxpr/ppermute | solution.py:19
  146.0 8.3 %collective-permute-start = (bf16[64,2048]{1,0:T(8,128)(2,1)S(1)}, bf16[64,2048]{1,0:T(8,128)(2,1)S(1)}, u32[]{:S(2)}, u32[]{:S(2)}) collective-permute-start(bf16[64,2048]{1,0:T(8,128)(2,1)S(1)} %fusion.69), channel_id=1, source_target_pairs={{0,1},{1,2},{2,3},{4,5},{5,6},{6,7},{8,9},{9,10},{10,11},{12,13},{... | collective-permute-start | bytes 786440 | tf_op jit(solution)/shard_map/while/body/eval_jaxpr/ppermute | solution.py:19
  160.6 8.3 %collective-permute-start = (bf16[64,2048]{1,0:T(8,128)(2,1)S(1)}, bf16[64,2048]{1,0:T(8,128)(2,1)S(1)}, u32[]{:S(2)}, u32[]{:S(2)}) collective-permute-start(bf16[64,2048]{1,0:T(8,128)(2,1)S(1)} %fusion.69), channel_id=1, source_target_pairs={{0,1},{1,2},{2,3},{4,5},{5,6},{6,7},{8,9},{9,10},{10,11},{12,13},{... | collective-permute-start | bytes 786440 | tf_op jit(solution)/shard_map/while/body/eval_jaxpr/ppermute | solution.py:19
  175.3 8.3 %collective-permute-start = (bf16[64,2048]{1,0:T(8,128)(2,1)S(1)}, bf16[64,2048]{1,0:T(8,128)(2,1)S(1)}, u32[]{:S(2)}, u32[]{:S(2)}) collective-permute-start(bf16[64,2048]{1,0:T(8,128)(2,1)S(1)} %fusion.69), channel_id=1, source_target_pairs={{0,1},{1,2},{2,3},{4,5},{5,6},{6,7},{8,9},{9,10},{10,11},{12,13},{... | collective-permute-start | bytes 786440 | tf_op jit(solution)/shard_map/while/body/eval_jaxpr/ppermute | solution.py:19
  196.6 8.7 %collective-permute-start.1 = (bf16[64,2048]{1,0:T(8,128)(2,1)S(1)}, bf16[64,2048]{1,0:T(8,128)(2,1)S(1)}, u32[]{:S(2)}, u32[]{:S(2)}) collective-permute-start(bf16[64,2048]{1,0:T(8,128)(2,1)S(1)} %fusion.74), channel_id=1, source_target_pairs={{1,0},{2,1},{3,2},{5,4},{6,5},{7,6},{9,8},{10,9},{11,10},{13,12},{... | collective-permute-start | bytes 786440 | tf_op jit(solution)/shard_map/while/body/eval_jaxpr/ppermute | solution.py:19
  217.2 8.3 %collective-permute-start.1 = (bf16[64,2048]{1,0:T(8,128)(2,1)S(1)}, bf16[64,2048]{1,0:T(8,128)(2,1)S(1)}, u32[]{:S(2)}, u32[]{:S(2)}) collective-permute-start(bf16[64,2048]{1,0:T(8,128)(2,1)S(1)} %fusion.74), channel_id=1, source_target_pairs={{1,0},{2,1},{3,2},{5,4},{6,5},{7,6},{9,8},{10,9},{11,10},{13,12},{... | collective-permute-start | bytes 786440 | tf_op jit(solution)/shard_map/while/body/eval_jaxpr/ppermute | solution.py:19
  237.3 8.3 %collective-permute-start.1 = (bf16[64,2048]{1,0:T(8,128)(2,1)S(1)}, bf16[64,2048]{1,0:T(8,128)(2,1)S(1)}, u32[]{:S(2)}, u32[]{:S(2)}) collective-permute-start(bf16[64,2048]{1,0:T(8,128)(2,1)S(1)} %fusion.74), channel_id=1, source_target_pairs={{1,0},{2,1},{3,2},{5,4},{6,5},{7,6},{9,8},{10,9},{11,10},{13,12},{... | collective-permute-start | bytes 786440 | tf_op jit(solution)/shard_map/while/body/eval_jaxpr/ppermute | solution.py:19
  257.4 8.3 %collective-permute-start.1 = (bf16[64,2048]{1,0:T(8,128)(2,1)S(1)}, bf16[64,2048]{1,0:T(8,128)(2,1)S(1)}, u32[]{:S(2)}, u32[]{:S(2)}) collective-permute-start(bf16[64,2048]{1,0:T(8,128)(2,1)S(1)} %fusion.74), channel_id=1, source_target_pairs={{1,0},{2,1},{3,2},{5,4},{6,5},{7,6},{9,8},{10,9},{11,10},{13,12},{... | collective-permute-start | bytes 786440 | tf_op jit(solution)/shard_map/while/body/eval_jaxpr/ppermute | solution.py:19
  277.5 8.3 %collective-permute-start.1 = (bf16[64,2048]{1,0:T(8,128)(2,1)S(1)}, bf16[64,2048]{1,0:T(8,128)(2,1)S(1)}, u32[]{:S(2)}, u32[]{:S(2)}) collective-permute-start(bf16[64,2048]{1,0:T(8,128)(2,1)S(1)} %fusion.74), channel_id=1, source_target_pairs={{1,0},{2,1},{3,2},{5,4},{6,5},{7,6},{9,8},{10,9},{11,10},{13,12},{... | collective-permute-start | bytes 786440 | tf_op jit(solution)/shard_map/while/body/eval_jaxpr/ppermute | solution.py:19
  297.6 8.3 %collective-permute-start.1 = (bf16[64,2048]{1,0:T(8,128)(2,1)S(1)}, bf16[64,2048]{1,0:T(8,128)(2,1)S(1)}, u32[]{:S(2)}, u32[]{:S(2)}) collective-permute-start(bf16[64,2048]{1,0:T(8,128)(2,1)S(1)} %fusion.74), channel_id=1, source_target_pairs={{1,0},{2,1},{3,2},{5,4},{6,5},{7,6},{9,8},{10,9},{11,10},{13,12},{... | collective-permute-start | bytes 786440 | tf_op jit(solution)/shard_map/while/body/eval_jaxpr/ppermute | solution.py:19
  317.6 8.3 %collective-permute-start.1 = (bf16[64,2048]{1,0:T(8,128)(2,1)S(1)}, bf16[64,2048]{1,0:T(8,128)(2,1)S(1)}, u32[]{:S(2)}, u32[]{:S(2)}) collective-permute-start(bf16[64,2048]{1,0:T(8,128)(2,1)S(1)} %fusion.74), channel_id=1, source_target_pairs={{1,0},{2,1},{3,2},{5,4},{6,5},{7,6},{9,8},{10,9},{11,10},{13,12},{... | collective-permute-start | bytes 786440 | tf_op jit(solution)/shard_map/while/body/eval_jaxpr/ppermute | solution.py:19
  332.8 1.0 copy-start.2
  332.8 1.2 copy-start.4
  332.8 1.4 copy-start.5
  332.8 71.3 %copy-start.3 = (bf16[1,256,2048]{2,1,0:T(8,128)(2,1)S(1)}, bf16[1,256,2048]{2,1,0:T(8,128)(2,1)}, u32[]{:S(2)}) copy-start(bf16[1,256,2048]{2,1,0:T(8,128)(2,1)} %param.12) | copy-start | bytes 3145732
Sparse Core Ops, SparseCore 0:
  21.3 56.9 all-gather.1
  332.9 71.1 reduce-scatter.1
where the time goes:
time: 416 us; the launch traced here: 414 us
  waiting for transfers between devices  184 us (44%)
  matrix products  122 us (29%)
  starting transfers between devices  39.1 us (9%)
  other arithmetic  37.6 us (9%)
  between operations  14.1 us (3%)
  local copies, waits for them, and re-layouts  8.54 us (2%)
  blocking collectives  7.66 us (2%)
    dot_general x14, matrix products, section_forward(): preact = jnp.dot(normed, masked, preferred_element_type=jnp.float32)  72.2 us
    ppermute x14, waiting for transfers between devices, shifted(): return lax.ppermute(block, axis, route)  67.1 us
    reduce_scatter x1, waiting for transfers between devices, body(): lax.psum_scatter(lax.dot_general(flat_normed, flat_grad, (((0,), (0,)), (...  60.3 us
    all_gather x1, waiting for transfers between devices, body(): masked = lax.all_gather(masked_shard, 'dp', axis=0, tiled=True)  56.9 us
    dot_general x7, matrix products, section_backward(): lax.dot_general(grad_pre, masked, (((1,), (1,)), ((), ())), preferred_ele...  43.1 us
    ppermute x14, starting transfers between devices, shifted(): return lax.ppermute(block, axis, route)  38.8 us
    dynamic_update_slice x14, other arithmetic, write_slot(): return lax.dynamic_update_index_in_dim(buffer, chosen, slot_index, 0)  20.3 us
  transfers between devices with their start and end apart: 16, of which 16 were waited for; matrix products, arithmetic and copies ran while one was open for 4% of the time, Pallas kernels for 0%

commit v1 on v0

--- a/solution.py
+++ b/solution.py
@@ -1,8 +1,11 @@
+import functools
 import math
 
 import jax
 import jax.numpy as jnp
 from jax import lax
+from jax.experimental import pallas as pl
+from jax.experimental.pallas import tpu as pltpu
 from jax.sharding import PartitionSpec as P
 
 epsilon = 1e-06
@@ -147,6 +150,408 @@
     return (gradient[None], flip_sum)
 
 
+def pick_chunk(rows):
+    return 32 if rows % 32 == 0 else 16
+
+
+def fused_fits(mesh, activations, weight):
+    replicas, sections = mesh.shape["dp"], mesh.shape["section"]
+    micro, batch, width = activations.shape
+    shard_rows = weight.shape[1] // replicas
+    rows = micro * batch // replicas
+    gathered = replicas // 2 * rows * width * 2
+    return (
+        replicas % 2 == 0
+        and replicas > 2
+        and sections > 1
+        and shard_rows % 128 == 0
+        and rows % 16 == 0
+        and width % 512 == 0
+        and gathered + 3 * width * width * 2 < 40 * 2**20
+    )
+
+
+def spread_matrix(count, transposed):
+    groups = count // 4
+    rows = lax.broadcasted_iota(jnp.int32, (count, count), 1 if transposed else 0)
+    columns = lax.broadcasted_iota(jnp.int32, (count, count), 0 if transposed else 1)
+    place = sum((columns >= groups * j).astype(jnp.int32) for j in (1, 2, 3))
+    hit = rows == 4 * (columns - groups * place) + place
+    return jnp.where(hit, 1.0, 0.0).astype(jnp.bfloat16)
+
+
+def fused_kernel(
+    chunk, tokens, act, cot, weight, gain, pairs, earlier, out, flips,
+    packed, full, hidden, normed, deriv, outgoing, upstream, downstream, grads, terms,
+    scaled, partial, incoming, counts,
+    pack_send, pack_recv, relay_send, relay_recv, fwd_send, fwd_recv, bwd_send, bwd_recv,
+    term_send, term_recv, grad_send, grad_recv, part_send, part_recv, flip_send, flip_recv, pair_sem,
+):
+    section = lax.axis_index("section")
+    sections = lax.axis_size("section")
+    me = lax.axis_index("dp")
+    chips = lax.axis_size("dp") // 2
+    chip = lax.div(me, 2)
+    core = lax.rem(me, 2)
+    sibling = 2 * chip + 1 - core
+    last = sections - 1
+    shard_rows, width = weight.shape
+    groups = shard_rows // 4
+    rows = hidden.shape[0]
+    steps = rows // chunk
+    tile = 512
+    tiles = width // tile
+    own_columns = pl.multiple_of(chip * 2 * shard_rows, 2 * shard_rows)
+
+    def peer_chip(k):
+        return lax.rem(chip + k, chips)
+
+    def at_dp(index):
+        return {"dp": index}
+
+    def remote(src, dst, send, recv, where):
+        return pltpu.make_async_remote_copy(
+            src_ref=src, dst_ref=dst, send_sem=send, recv_sem=recv,
+            device_id=where, device_id_type=pl.DeviceIdType.MESH,
+        )
+
+    barrier = pltpu.get_barrier_semaphore()
+
+    def greet(where):
+        pl.semaphore_signal(barrier, inc=1, device_id=where, device_id_type=pl.DeviceIdType.MESH)
+
+    for k in range(1, chips):
+        greet(at_dp(2 * peer_chip(k) + core))
+    greet(at_dp(sibling))
+
+    @pl.when(section > 0)
+    def _():
+        greet({"section": section - 1})
+
+    @pl.when(section < last)
+    def _():
+        greet({"section": section + 1})
+
+    own_pairs = pairs.at[pl.ds(pl.multiple_of(me * groups, groups), groups), :]
+    gather_rows = spread_matrix(shard_rows, True)
+    for t in range(tiles):
+        cols = slice(t * tile, (t + 1) * tile)
+        split = jnp.dot(gather_rows, weight[:, cols], preferred_element_type=jnp.float32)
+        w0, w1, w2, w3 = (split[j * groups:(j + 1) * groups] for j in range(4))
+        p = own_pairs[:, cols]
+        first = jnp.where(p <= 2, w0, jnp.where(p <= 4, w1, w2))
+        second = jnp.where(p == 0, w1, jnp.where((p == 1) | (p == 3), w2, w3))
+        packed[me, 0:groups, cols] = first.astype(jnp.bfloat16)
+        packed[me, groups:2 * groups, cols] = second.astype(jnp.bfloat16)
+
+    pl.semaphore_wait(barrier, chips + (section > 0).astype(jnp.int32) + (section < last).astype(jnp.int32))
+
+    def pack_copy(k, source):
+        slot = packed.at[2 * source + core]
+        return remote(slot, slot, pack_send.at[k], pack_recv.at[source], at_dp(2 * peer_chip(k) + core))
+
+    def relay_copy(source, parity):
+        slot = packed.at[2 * source + parity]
+        return remote(slot, slot, relay_send.at[source], relay_recv.at[source], at_dp(sibling))
+
+    for k in range(1, chips):
+        pack_copy(k, chip).start()
+    relay_copy(chip, core).start()
+
+    p = own_pairs[...]
+    q = earlier[...]
+    changed = jnp.where(p == q, 0, jnp.where(p + q == 5, 4, 2))
+    total = jnp.zeros((8, 128), jnp.int32)
+    for a in range(groups // 8):
+        for b in range(width // 128):
+            total = total + changed[a * 8:(a + 1) * 8, b * 128:(b + 1) * 128]
+    counts[chip] = total
+
+    def flip_copy(k, source):
+        slot = counts.at[source]
+        return remote(slot, slot, flip_send.at[k], flip_recv.at[source], at_dp(2 * peer_chip(k) + core))
+
+    for k in range(1, chips):
+        flip_copy(k, chip).start()
+
+    spread_rows = spread_matrix(shard_rows, False)
+
+    def unpack(owner):
+        owned = pl.multiple_of(owner * groups, groups)
+        target = pl.multiple_of(owner * shard_rows, shard_rows)
+        for t in range(tiles):
+            cols = slice(t * tile, (t + 1) * tile)
+            p = pairs[pl.ds(owned, groups), cols]
+            v0 = packed[owner, 0:groups, cols].astype(jnp.float32)
+            v1 = packed[owner, groups:2 * groups, cols].astype(jnp.float32)
+            zero = jnp.zeros_like(v0)
+            parts = (
+                jnp.where(p <= 2, v0, zero),
+                jnp.where((p == 3) | (p == 4), v0, jnp.where(p == 0, v1, zero)),
+                jnp.where(p == 5, v0, jnp.where((p == 1) | (p == 3), v1, zero)),
+                jnp.where((p == 2) | (p >= 4), v1, zero),
+            )
+            stacked = jnp.concatenate(parts, axis=0).astype(jnp.bfloat16)
+            spread = jnp.dot(spread_rows, stacked, preferred_element_type=jnp.float32)
+            full[pl.ds(target, shard_rows), cols] = spread.astype(jnp.bfloat16)
+
+    def receive(k, carry):
+        source = lax.rem(chip + k, chips)
+
+        @pl.when(k > 0)
+        def _():
+            pack_copy(1, source).wait_recv()
+            relay_copy(source, core).start()
+
+        unpack(2 * source + core)
+        relay_copy(source, 1 - core).wait_recv()
+        unpack(2 * source + 1 - core)
+        return carry
+
+    lax.fori_loop(0, chips, receive, 0)
+
+    @pl.when(section == 0)
+    def _():
+        for m in range(act.shape[0]):
+            hidden[m * act.shape[1]:(m + 1) * act.shape[1], :] = act[m]
+
+    @pl.when(section == last)
+    def _():
+        for m in range(cot.shape[0]):
+            upstream[m * cot.shape[1]:(m + 1) * cot.shape[1], :] = cot[m]
+
+    def span(i):
+        return pl.ds(pl.multiple_of(i * chunk, chunk), chunk)
+
+    def fwd_copy(i):
+        return remote(outgoing.at[span(i)], hidden.at[span(i)], fwd_send.at[i], fwd_recv.at[i], {"section": section + 1})
+
+    def fwd_arrival(i):
+        return remote(outgoing.at[span(i)], hidden.at[span(i)], fwd_send.at[i], fwd_recv.at[i], {"section": section})
+
+    def bwd_copy(i):
+        return remote(downstream.at[span(i)], upstream.at[span(i)], bwd_send.at[i], bwd_recv.at[i], {"section": section - 1})
+
+    def bwd_arrival(i):
+        return remote(downstream.at[span(i)], upstream.at[span(i)], bwd_send.at[i], bwd_recv.at[i], {"section": section})
+
+    def term_copy(k, i):
+        peer = peer_chip(k)
+        wanted = pl.ds(pl.multiple_of(peer * 2 * shard_rows, 2 * shard_rows), 2 * shard_rows)
+        return remote(
+            normed.at[span(i), wanted], terms.at[chip, span(i)],
+            term_send.at[k, i], term_recv.at[chip, i], at_dp(2 * peer + core),
+        )
+
+    def grad_copy(k, i):
+        return remote(
+            grads.at[chip, span(i)], grads.at[chip, span(i)],
+            grad_send.at[k, i], grad_recv.at[chip, i], at_dp(2 * peer_chip(k) + core),
+        )
+
+    def forward(i):
+        @pl.when(section > 0)
+        def _():
+            fwd_arrival(i).wait_recv()
+
+        values = hidden[span(i)].astype(jnp.float32)
+        scale = lax.rsqrt(jnp.mean(values * values, axis=-1, keepdims=True) + epsilon)
+        rounded = (values * scale * gain[...]).astype(jnp.bfloat16)
+        normed[span(i)] = rounded
+        for t in range(tiles):
+            cols = slice(t * tile, (t + 1) * tile)
+            preact = jnp.dot(rounded, full[:, cols], preferred_element_type=jnp.float32)
+            cdf = 0.5 * (1.0 + lax.erf(preact * half_root))
+            pdf = jnp.exp(-0.5 * preact * preact) * density_scale
+            deriv[span(i), cols] = cdf + preact * pdf
+            outgoing[span(i), cols] = (values[:, cols] + preact * cdf).astype(jnp.bfloat16)
+
+        @pl.when(section < last)
+        def _():
+            fwd_copy(i).start()
+
+        terms[chip, span(i)] = normed[span(i), pl.ds(own_columns, 2 * shard_rows)]
+        for k in range(1, chips):
+            term_copy(k, i).start()
+
+    def backward(i):
+        @pl.when(section < last)
+        def _():
+            bwd_arrival(i).wait_recv()
+
+        above = upstream[span(i)].astype(jnp.float32)
+        grad_pre = (above * deriv[span(i)]).astype(jnp.bfloat16)
+        grads[chip, span(i)] = grad_pre
+        for k in range(1, chips):
+            grad_copy(k, i).start()
+
+        @pl.when(section > 0)
+        def _():
+            values = hidden[span(i)].astype(jnp.float32)
+            scale = lax.rsqrt(jnp.mean(values * values, axis=-1, keepdims=True) + epsilon)
+            along = jnp.zeros((chunk, 1), jnp.float32)
+            for t in range(tiles):
+                cols = slice(t * tile, (t + 1) * tile)
+                piece = lax.dot_general(
+                    grad_pre, full[cols, :], (((1,), (1,)), ((), ())), preferred_element_type=jnp.float32
+                ) * gain[:, cols]
+                scaled[:, cols] = piece
+                along = along + jnp.sum(piece * values[:, cols], axis=-1, keepdims=True)
+            pull = scale * scale * scale * (along / width)
+            result = upstream[span(i)].astype(jnp.float32) + scale * scaled[...] - values * pull
+            downstream[span(i)] = result.astype(jnp.bfloat16)
+            bwd_copy(i).start()
+
+    def step(k, carry):
+        at_last = (section == last).astype(jnp.int32)
+        half = lax.div(k, 2)
+        goes_back = at_last * lax.rem(k, 2) + (1 - at_last) * lax.div(k, steps)
+        index = at_last * half + (1 - at_last) * lax.rem(k, steps)
+
+        @pl.when(goes_back == 0)
+        def _():
+            forward(index)
+
+        @pl.when(goes_back == 1)
+        def _():
+            backward(index)
+
+        return carry
+
+    lax.fori_loop(0, 2 * steps, step, 0)
+
+    def arrivals(i, carry):
+        for k in range(1, chips):
+            source = peer_chip(k)
+            remote(
+                terms.at[source, span(i)], terms.at[source, span(i)],
+                term_send.at[k, i], term_recv.at[source, i], at_dp(me),
+            ).wait_recv()
+            remote(
+                grads.at[source, span(i)], grads.at[source, span(i)],
+                grad_send.at[k, i], grad_recv.at[source, i], at_dp(me),
+            ).wait_recv()
+        return carry
+
+    lax.fori_loop(0, steps, arrivals, 0)
+
+    def product(half, cols):
+        left = pl.ds(pl.multiple_of(half * shard_rows, shard_rows), shard_rows)
+        total = jnp.zeros((shard_rows, tile), jnp.float32)
+        for c in range(chips):
+            total = total + lax.dot_general(
+                terms[c, :, left], grads[c, :, cols], (((0,), (0,)), ((), ())), preferred_element_type=jnp.float32
+            )
+        return total
+
+    def part_copy(t):
+        return remote(partial.at[t], incoming.at[t], part_send.at[t], part_recv.at[t], at_dp(sibling))
+
+    for t in range(tiles):
+        partial[t] = product(1 - core, slice(t * tile, (t + 1) * tile)).astype(jnp.bfloat16)
+        part_copy(t).start()
+    own_rows = pl.ds(pl.multiple_of(me * shard_rows, shard_rows), shard_rows)
+    for t in range(tiles):
+        cols = slice(t * tile, (t + 1) * tile)
+        pruned = weight[:, cols].astype(jnp.float32) - full[own_rows, cols].astype(jnp.float32)
+        out[:, cols] = product(core, cols) * (1.0 / math.sqrt(tokens)) + decay_rate * pruned
+
+    for k in range(1, chips):
+        flip_copy(k, peer_chip(k)).wait_recv()
+    total = counts[0]
+    for c in range(1, chips):
+        total = total + counts[c]
+    counts[chips] = total
+    pair_copy = remote(counts.at[chips], counts.at[chips + 1], pair_sem.at[0], pair_sem.at[1], at_dp(sibling))
+    pair_copy.start()
+
+    for t in range(tiles):
+        cols = slice(t * tile, (t + 1) * tile)
+        part_copy(t).wait_recv()
+        out[:, cols] = out[:, cols] + incoming[t].astype(jnp.float32) * (1.0 / math.sqrt(tokens))
+    pair_copy.wait_recv()
+    flips[...] = counts[chips] + counts[chips + 1]
+
+    pair_copy.wait_send()
+    for t in range(tiles):
+        part_copy(t).wait_send()
+    for k in range(1, chips):
+        pack_copy(k, chip).wait_send()
+        flip_copy(k, chip).wait_send()
+
+    for c in range(chips):
+        relay_copy(c, core).wait_send()
+
+    def drain(i, carry):
+        for k in range(1, chips):
+            term_copy(k, i).wait_send()
+            grad_copy(k, i).wait_send()
+
+        @pl.when(section < last)
+        def _():
+            fwd_copy(i).wait_send()
+
+        @pl.when(section > 0)
+        def _():
+            bwd_copy(i).wait_send()
+
+        return carry
+
+    lax.fori_loop(0, steps, drain, 0)
+
+
+def fused_body(activations, cotangent, weight, norm_gain, pair_mask, earlier_mask):
+    replicas = lax.axis_size("dp")
+    chips = replicas // 2
+    micro, micro_rows, width = activations.shape
+    shard_rows = weight.shape[1]
+    groups = shard_rows // 4
+    rows = micro * micro_rows
+    chunk = pick_chunk(rows)
+    steps = rows // chunk
+    tile = 512
+    tiles = width // tile
+    bf, f32 = jnp.bfloat16, jnp.float32
+    dma = pltpu.SemaphoreType.DMA
+    vmem = pl.BlockSpec(memory_space=pltpu.VMEM)
+    gradient, flips = pl.pallas_call(
+        functools.partial(fused_kernel, chunk, rows * replicas),
+        out_shape=(
+            jax.ShapeDtypeStruct((shard_rows, width), f32),
+            jax.ShapeDtypeStruct((8, 128), jnp.int32),
+        ),
+        in_specs=[vmem] * 6,
+        out_specs=(vmem, vmem),
+        scratch_shapes=[
+            pltpu.VMEM((replicas, 2 * groups, width), bf),
+            pltpu.VMEM((width, width), bf),
+            pltpu.VMEM((rows, width), bf),
+            pltpu.VMEM((rows, width), bf),
+            pltpu.VMEM((rows, width), f32),
+            pltpu.VMEM((rows, width), bf),
+            pltpu.VMEM((rows, width), bf),
+            pltpu.VMEM((rows, width), bf),
+            pltpu.VMEM((chips, rows, width), bf),
+            pltpu.VMEM((chips, rows, 2 * shard_rows), bf),
+            pltpu.VMEM((chunk, width), f32),
+            pltpu.VMEM((tiles, shard_rows, tile), bf),
+            pltpu.VMEM((tiles, shard_rows, tile), bf),
+            pltpu.VMEM((chips + 2, 8, 128), jnp.int32),
+            dma((chips,)), dma((chips,)), dma((chips,)), dma((chips,)),
+            dma((steps,)), dma((steps,)), dma((steps,)), dma((steps,)),
+            dma((chips, steps)), dma((chips, steps)), dma((chips, steps)), dma((chips, steps)),
+            dma((tiles,)), dma((tiles,)), dma((chips,)), dma((chips,)), dma((2,)),
+        ],
+        compiler_params=pltpu.CompilerParams(
+            collective_id=0, has_side_effects=True, vmem_limit_bytes=60 * 2**20
+        ),
+        name="fused_step",
+    )(
+        activations, cotangent, weight[0], norm_gain, pair_mask[0], earlier_mask[0],
+    )
+    return (gradient[None], jnp.sum(flips).reshape(1))
+
+
 def solution(mesh):
     placed = (
         P(None, "dp", None),
@@ -156,10 +561,15 @@
         P("section", None, None),
         P("section", "dp", None),
     )
-    return jax.shard_map(
-        body,
-        mesh=mesh,
-        in_specs=placed,
-        out_specs=(P("section", "dp", None), P("section")),
-        check_vma=False,
-    )
+
+    def step(*arrays):
+        chosen = fused_body if fused_fits(mesh, arrays[0], arrays[2]) else body
+        return jax.shard_map(
+            chosen,
+            mesh=mesh,
+            in_specs=placed,
+            out_specs=(P("section", "dp", None), P("section")),
+            check_vma=False,
+        )(*arrays)
+
+    return step

time: 416 us -> 145 us (0.35)
  waiting for transfers between devices: 184 us -> 0 us
  Pallas kernels: 0 us -> 139 us
  matrix products: 122 us -> 0 us
  starting transfers between devices: 39.1 us -> 0 us
  other arithmetic: 37.6 us -> 1.32 us
  between operations: 14.1 us -> 0.64 us
  blocking collectives: 7.66 us -> 0 us
  local copies, waits for them, and re-layouts: 8.54 us -> 3.13 us
    pallas_call x0 -> x1, Pallas kernels: none -> 139 us  [fused_body(): pl.pallas_call(functools.partial(fused_kernel, chunk, rows * replicas), o...]
    dot_general x22 -> x0, matrix products: 122 us -> none  [the longest x14 72.2 us: section_forward(): preact = jnp.dot(normed, masked, preferred_element_type=jnp.float32)]
    ppermute x14 -> x0, waiting for transfers between devices: 67.1 us -> none  [shifted(): return lax.ppermute(block, axis, route)]
    reduce_scatter x1 -> x0, waiting for transfers between devices: 60.3 us -> none  [body(): lax.psum_scatter(lax.dot_general(flat_normed, flat_grad, (((0,), (0,)), (...]
    all_gather x1 -> x0, waiting for transfers between devices: 56.9 us -> none  [body(): masked = lax.all_gather(masked_shard, 'dp', axis=0, tiled=True)]
    ppermute x14 -> x0, starting transfers between devices: 38.8 us -> none  [shifted(): return lax.ppermute(block, axis, route)]
    dynamic_update_slice x14 -> x0, other arithmetic: 20.3 us -> none  [write_slot(): return lax.dynamic_update_index_in_dim(buffer, chosen, slot_index, 0)]
    select_n x3 -> x0, other arithmetic: 8.31 us -> none  [the longest x1 4.46 us: body(): masked_shard = jnp.where(own_kept, own_weight, jnp.zeros_like(own_weight))]
  transfers between devices with their start and end apart: 16 -> 0, of which waited for: 16 -> 0; matrix products, arithmetic and copies ran while one was open for 4% -> 0% of each run, Pallas kernels for 0% -> 0%
where the time goes in v1:
time: 145 us
  Pallas kernels  139 us (96%)
  local copies, waits for them, and re-layouts  3.13 us (2%)
    pallas_call x1, Pallas kernels, fused_body(): pl.pallas_call(functools.partial(fused_kernel, chunk, rows * replicas), o...  139 us
    unnamed x1, local copies, waits for them, and re-layouts  3.13 us

profile of v1, /device:TPU:0, one launch (start us, length us, event | category | flops | bytes accessed | tf_op | source)
XLA Modules:
  0.0 144.5 jit_solution(3908898686815144562)
XLA Ops:
  0.6 139.4 %fused_step.1 = (f32[256,2048]{1,0:T(8,128)}, s32[8,128]{1,0:T(8,128)}) custom-call(bf16[4,64,2048]{2,1,0:T(8,128)(2,1)} %act.1, bf16[4,64,2048]{2,1,0:T(8,128)(2,1)} %cot.1, bf16[256,2048]{1,0:T(8,128)(2,1)} %bitcast.7, f32[1,2048]{1,0:T(1,128)} %gain.1, s32[512,2048]{1,0:T(8,128)} %bitcast.5, s32[64,2048]{1,0:T(8,128)} %bitcast.8), custom_call_target="tpu_custom_call" | custom-call | tf_op jit(solution)/shard_map/fused_step/pallas_call | solution.py:517
  140.1 1.3 reduce_sum.9
  141.4 3.1 %copy.9 = f32[1,256,2048]{2,1,0:T(8,128)} copy(f32[1,256,2048]{2,1,0:T(8,128)} %bitcast.6) | data formatting | bytes 4194304

commit v2 on v1

--- a/solution.py
+++ b/solution.py
@@ -150,6 +150,9 @@
     return (gradient[None], flip_sum)
 
 
+HALVES = (0, 1)
+
+
 def pick_chunk(rows):
     return 32 if rows % 32 == 0 else 16
 
@@ -162,7 +165,7 @@
     gathered = replicas // 2 * rows * width * 2
     return (
         replicas % 2 == 0
-        and replicas > 2
+        and replicas == 2 * len(HALVES) ** 2
         and sections > 1
         and shard_rows % 128 == 0
         and rows % 16 == 0
@@ -181,9 +184,9 @@
 
 
 def fused_kernel(
-    chunk, tokens, act, cot, weight, gain, pairs, earlier, out, flips,
+    chunk, tokens, act, cot, weight, gain, pairs_hbm, earlier, out, flips,
     packed, full, hidden, normed, deriv, outgoing, upstream, downstream, grads, terms,
-    scaled, partial, incoming, counts,
+    scaled, partial, incoming, counts, pairs, own_pairs, load_sem, row_sem,
     pack_send, pack_recv, relay_send, relay_recv, fwd_send, fwd_recv, bwd_send, bwd_recv,
     term_send, term_recv, grad_send, grad_recv, part_send, part_recv, flip_send, flip_recv, pair_sem,
 ):
@@ -201,6 +204,10 @@
     steps = rows // chunk
     tile = 512
     tiles = width // tile
+    across = chip + 1 - 2 * lax.rem(chip, 2)
+    along_y = lax.rem(chip + 2, chips)
+    corner = lax.rem(across + 2, chips)
+    near = (across, along_y)
     own_columns = pl.multiple_of(chip * 2 * shard_rows, 2 * shard_rows)
 
     def peer_chip(k):
@@ -232,7 +239,31 @@
     def _():
         greet({"section": section + 1})
 
-    own_pairs = pairs.at[pl.ds(pl.multiple_of(me * groups, groups), groups), :]
+    own_load = pltpu.make_async_copy(
+        pairs_hbm.at[pl.ds(pl.multiple_of(me * groups, groups), groups), :], own_pairs, load_sem.at[0]
+    )
+    own_load.start()
+    all_load = pltpu.make_async_copy(pairs_hbm, pairs, load_sem.at[1])
+    all_load.start()
+    micro_rows = act.shape[1]
+
+    def row_loads(source, target):
+        return [
+            pltpu.make_async_copy(source.at[m], target.at[pl.ds(m * micro_rows, micro_rows)], row_sem.at[m])
+            for m in range(act.shape[0])
+        ]
+
+    @pl.when(section == 0)
+    def _():
+        for load in row_loads(act, hidden):
+            load.start()
+
+    @pl.when(section == last)
+    def _():
+        for load in row_loads(cot, upstream):
+            load.start()
+
+    own_load.wait()
     gather_rows = spread_matrix(shard_rows, True)
     for t in range(tiles):
         cols = slice(t * tile, (t + 1) * tile)
@@ -246,16 +277,29 @@
 
     pl.semaphore_wait(barrier, chips + (section > 0).astype(jnp.int32) + (section < last).astype(jnp.int32))
 
-    def pack_copy(k, source):
-        slot = packed.at[2 * source + core]
-        return remote(slot, slot, pack_send.at[k], pack_recv.at[source], at_dp(2 * peer_chip(k) + core))
+    def half_rows(h):
+        return pl.ds(h * groups, groups)
+
+    def pack_copy(way, source, h, route):
+        slot = packed.at[2 * source + core, half_rows(h)]
+        return remote(slot, slot, pack_send.at[route, h], pack_recv.at[source, h], at_dp(2 * near[way] + core))
+
+    def pack_own(way, h):
+        return pack_copy(way, chip, h, way)
+
+    def pack_onward(way):
+        return pack_copy(1 - way, near[way], way, 2)
+
+    def pack_arrival(source, h):
+        return pack_copy(0, source, h, 0)
 
     def relay_copy(source, parity):
         slot = packed.at[2 * source + parity]
         return remote(slot, slot, relay_send.at[source], relay_recv.at[source], at_dp(sibling))
 
-    for k in range(1, chips):
-        pack_copy(k, chip).start()
+    for h in HALVES:
+        for way in (0, 1):
+            pack_own(way, h if way == 0 else 1 - h).start()
     relay_copy(chip, core).start()
 
     p = own_pairs[...]
@@ -295,30 +339,43 @@
             spread = jnp.dot(spread_rows, stacked, preferred_element_type=jnp.float32)
             full[pl.ds(target, shard_rows), cols] = spread.astype(jnp.bfloat16)
 
-    def receive(k, carry):
-        source = lax.rem(chip + k, chips)
-
-        @pl.when(k > 0)
-        def _():
-            pack_copy(1, source).wait_recv()
-            relay_copy(source, core).start()
-
-        unpack(2 * source + core)
-        relay_copy(source, 1 - core).wait_recv()
-        unpack(2 * source + 1 - core)
-        return carry
-
-    lax.fori_loop(0, chips, receive, 0)
+    all_load.wait()
+
+    def unpack_two(first, second):
+        def one(k, carry):
+            unpack(jnp.where(k == 0, first, second))
+            return carry
+
+        lax.fori_loop(0, 2, one, 0)
+
+    relay_copy(chip, 1 - core).wait_recv()
+    unpack_two(2 * chip + core, 2 * chip + 1 - core)
+    for way in (0, 1):
+        pack_arrival(near[way], way).wait_recv()
+        pack_onward(way).start()
+    for way in (0, 1):
+        pack_arrival(near[way], 1 - way).wait_recv()
+        relay_copy(near[way], core).start()
+    unpack_two(2 * across + core, 2 * along_y + core)
+    for way in (0, 1):
+        relay_copy(near[way], 1 - core).wait_recv()
+    unpack_two(2 * across + 1 - core, 2 * along_y + 1 - core)
+    for h in HALVES:
+        pack_arrival(corner, h).wait_recv()
+    relay_copy(corner, core).start()
+    unpack_two_first = 2 * corner + core
+    relay_copy(corner, 1 - core).wait_recv()
+    unpack_two(unpack_two_first, 2 * corner + 1 - core)
 
     @pl.when(section == 0)
     def _():
-        for m in range(act.shape[0]):
-            hidden[m * act.shape[1]:(m + 1) * act.shape[1], :] = act[m]
+        for load in row_loads(act, hidden):
+            load.wait()
 
     @pl.when(section == last)
     def _():
-        for m in range(cot.shape[0]):
-            upstream[m * cot.shape[1]:(m + 1) * cot.shape[1], :] = cot[m]
+        for load in row_loads(cot, upstream):
+            load.wait()
 
     def span(i):
         return pl.ds(pl.multiple_of(i * chunk, chunk), chunk)
@@ -343,11 +400,25 @@
             term_send.at[k, i], term_recv.at[chip, i], at_dp(2 * peer + core),
         )
 
-    def grad_copy(k, i):
+    def grad_copy(way, source, h, route, i):
+        slot = grads.at[source, span(i), pl.ds(h * (width // 2), width // 2)]
         return remote(
-            grads.at[chip, span(i)], grads.at[chip, span(i)],
-            grad_send.at[k, i], grad_recv.at[chip, i], at_dp(2 * peer_chip(k) + core),
+            slot, slot, grad_send.at[route * 2 + h, i], grad_recv.at[source * 2 + h, i], at_dp(2 * near[way] + core)
         )
+
+    def grad_own(way, h, i):
+        return grad_copy(way, chip, h, way, i)
+
+    def grad_onward(way, i):
+        return grad_copy(1 - way, near[way], way, 2, i)
+
+    def grad_arrival(source, h, i):
+        return grad_copy(0, source, h, 0, i)
+
+    def pass_on(i):
+        for way in (0, 1):
+            grad_arrival(near[way], way, i).wait_recv()
+            grad_onward(way, i).start()
 
     def forward(i):
         @pl.when(section > 0)
@@ -374,6 +445,8 @@
         for k in range(1, chips):
             term_copy(k, i).start()
 
+    lag = min(2, steps)
+
     def backward(i):
         @pl.when(section < last)
         def _():
@@ -382,8 +455,13 @@
         above = upstream[span(i)].astype(jnp.float32)
         grad_pre = (above * deriv[span(i)]).astype(jnp.bfloat16)
         grads[chip, span(i)] = grad_pre
-        for k in range(1, chips):
-            grad_copy(k, i).start()
+        for h in HALVES:
+            for way in (0, 1):
+                grad_own(way, h if way == 0 else 1 - h, i).start()
+
+        @pl.when(i >= lag)
+        def _():
+            pass_on(i - lag)
 
         @pl.when(section > 0)
         def _():
@@ -427,11 +505,14 @@
                 terms.at[source, span(i)], terms.at[source, span(i)],
                 term_send.at[k, i], term_recv.at[source, i], at_dp(me),
             ).wait_recv()
-            remote(
-                grads.at[source, span(i)], grads.at[source, span(i)],
-                grad_send.at[k, i], grad_recv.at[source, i], at_dp(me),
-            ).wait_recv()
+        for way in (0, 1):
+            grad_arrival(near[way], 1 - way, i).wait_recv()
+        for h in HALVES:
+            grad_arrival(corner, h, i).wait_recv()
         return carry
+
+    for i in range(steps - lag, steps):
+        pass_on(i)
 
     lax.fori_loop(0, steps, arrivals, 0)
 
@@ -476,16 +557,22 @@
     for t in range(tiles):
         part_copy(t).wait_send()
     for k in range(1, chips):
-        pack_copy(k, chip).wait_send()
         flip_copy(k, chip).wait_send()
 
+    for way in (0, 1):
+        pack_onward(way).wait_send()
+        for h in HALVES:
+            pack_own(way, h).wait_send()
     for c in range(chips):
         relay_copy(c, core).wait_send()
 
     def drain(i, carry):
         for k in range(1, chips):
             term_copy(k, i).wait_send()
-            grad_copy(k, i).wait_send()
+        for way in (0, 1):
+            grad_onward(way, i).wait_send()
+            for h in HALVES:
+                grad_own(way, h, i).wait_send()
 
         @pl.when(section < last)
         def _():
@@ -514,13 +601,14 @@
     bf, f32 = jnp.bfloat16, jnp.float32
     dma = pltpu.SemaphoreType.DMA
     vmem = pl.BlockSpec(memory_space=pltpu.VMEM)
+    hbm = pl.BlockSpec(memory_space=pl.ANY)
     gradient, flips = pl.pallas_call(
         functools.partial(fused_kernel, chunk, rows * replicas),
         out_shape=(
             jax.ShapeDtypeStruct((shard_rows, width), f32),
             jax.ShapeDtypeStruct((8, 128), jnp.int32),
         ),
-        in_specs=[vmem] * 6,
+        in_specs=[hbm, hbm, vmem, vmem, hbm, vmem],
         out_specs=(vmem, vmem),
         scratch_shapes=[
             pltpu.VMEM((replicas, 2 * groups, width), bf),
@@ -537,9 +625,12 @@
             pltpu.VMEM((tiles, shard_rows, tile), bf),
             pltpu.VMEM((tiles, shard_rows, tile), bf),
             pltpu.VMEM((chips + 2, 8, 128), jnp.int32),
-            dma((chips,)), dma((chips,)), dma((chips,)), dma((chips,)),
+            pltpu.VMEM((width // 4, width), jnp.int32),
+            pltpu.VMEM((groups, width), jnp.int32),
+            dma((2,)), dma((micro,)),
+            dma((3, 2)), dma((chips, 2)), dma((chips,)), dma((chips,)),
             dma((steps,)), dma((steps,)), dma((steps,)), dma((steps,)),
-            dma((chips, steps)), dma((chips, steps)), dma((chips, steps)), dma((chips, steps)),
+            dma((chips, steps)), dma((chips, steps)), dma((6, steps)), dma((2 * chips, steps)),
             dma((tiles,)), dma((tiles,)), dma((chips,)), dma((chips,)), dma((2,)),
         ],
         compiler_params=pltpu.CompilerParams(

time: 145 us -> 124 us (0.86)
  Pallas kernels: 139 us -> 119 us
    pallas_call x1, Pallas kernels: 139 us -> 119 us  [fused_body(): pl.pallas_call(functools.partial(fused_kernel, chunk, rows * replicas), o...]
where the time goes in v2:
time: 124 us
  Pallas kernels  119 us (96%)
  local copies, waits for them, and re-layouts  3.13 us (3%)
  other arithmetic  1.32 us (1%)
    pallas_call x1, Pallas kernels, fused_body(): pl.pallas_call(functools.partial(fused_kernel, chunk, rows * replicas), o...  119 us
    unnamed x1, local copies, waits for them, and re-layouts  3.13 us

profile of v2, /device:TPU:0, one launch (start us, length us, event | category | flops | bytes accessed | tf_op | source)
XLA Modules:
  0.0 123.8 jit_solution(14115394966252993334)
XLA Ops:
  0.6 118.7 %fused_step.1 = (f32[256,2048]{1,0:T(8,128)}, s32[8,128]{1,0:T(8,128)}) custom-call(bf16[4,64,2048]{2,1,0:T(8,128)(2,1)} %act.1, bf16[4,64,2048]{2,1,0:T(8,128)(2,1)} %cot.1, bf16[256,2048]{1,0:T(8,128)(2,1)} %bitcast.7, f32[1,2048]{1,0:T(1,128)} %gain.1, s32[512,2048]{1,0:T(8,128)} %bitcast.5, s32[64,2048]{1,0:T(8,128)} %bitcast.8), custom_call_target="tpu_custom_call" | custom-call | tf_op jit(solution)/shard_map/fused_step/pallas_call | solution.py:605
  119.3 1.3 %reduce_sum.9 = s32[]{:T(128)} reduce(s32[8,128]{1,0:T(8,128)} %get-tuple-element.5, s32[]{:T(128)} %constant.0.clone.1), dimensions={0,1}, to_apply=%region_0.0 | reduce | flops 1023 | bytes 4104 | tf_op jit(solution)/shard_map/reduce_sum | solution.py:643
  120.6 3.1 %copy.9 = f32[1,256,2048]{2,1,0:T(8,128)} copy(f32[1,256,2048]{2,1,0:T(8,128)} %bitcast.6) | data formatting | bytes 4194304

commit v3 on v2

--- a/solution.py
+++ b/solution.py
@@ -186,7 +186,7 @@
 def fused_kernel(
     chunk, tokens, act, cot, weight, gain, pairs_hbm, earlier, out, flips,
     packed, full, hidden, normed, deriv, outgoing, upstream, downstream, grads, terms,
-    scaled, partial, incoming, counts, pairs, own_pairs, load_sem, row_sem,
+    scaled, partial, incoming, counts, pairs, own_pairs, load_sem, row_sem, turned, result_tiles, out_sem,
     pack_send, pack_recv, relay_send, relay_recv, fwd_send, fwd_recv, bwd_send, bwd_recv,
     term_send, term_recv, grad_send, grad_recv, part_send, part_recv, flip_send, flip_recv, pair_sem,
 ):
@@ -377,6 +377,17 @@
         for load in row_loads(cot, upstream):
             load.wait()
 
+    @pl.when(section == last)
+    def _():
+        def turn(r, carry):
+            block = pl.ds(pl.multiple_of(r * shard_rows, shard_rows), shard_rows)
+            for t in range(tiles):
+                cols = slice(t * tile, (t + 1) * tile)
+                turned[cols, block] = full[block, cols].T
+            return carry
+
+        lax.fori_loop(0, 2 * chips, turn, 0)
+
     def span(i):
         return pl.ds(pl.multiple_of(i * chunk, chunk), chunk)
 
@@ -467,14 +478,26 @@
         def _():
             values = hidden[span(i)].astype(jnp.float32)
             scale = lax.rsqrt(jnp.mean(values * values, axis=-1, keepdims=True) + epsilon)
-            along = jnp.zeros((chunk, 1), jnp.float32)
-            for t in range(tiles):
-                cols = slice(t * tile, (t + 1) * tile)
-                piece = lax.dot_general(
-                    grad_pre, full[cols, :], (((1,), (1,)), ((), ())), preferred_element_type=jnp.float32
-                ) * gain[:, cols]
-                scaled[:, cols] = piece
-                along = along + jnp.sum(piece * values[:, cols], axis=-1, keepdims=True)
+            def pull_back(is_turned):
+                for t in range(tiles):
+                    cols = slice(t * tile, (t + 1) * tile)
+                    if is_turned:
+                        piece = jnp.dot(grad_pre, turned[:, cols], preferred_element_type=jnp.float32)
+                    else:
+                        piece = lax.dot_general(
+                            grad_pre, full[cols, :], (((1,), (1,)), ((), ())), preferred_element_type=jnp.float32
+                        )
+                    scaled[:, cols] = piece * gain[:, cols]
+
+            @pl.when(section == last)
+            def _():
+                pull_back(True)
+
+            @pl.when(section < last)
+            def _():
+                pull_back(False)
+
+            along = jnp.sum(scaled[...] * values, axis=-1, keepdims=True)
             pull = scale * scale * scale * (along / width)
             result = upstream[span(i)].astype(jnp.float32) + scale * scaled[...] - values * pull
             downstream[span(i)] = result.astype(jnp.bfloat16)
@@ -525,6 +548,9 @@
             )
         return total
 
+    def out_copy(t):
+        return pltpu.make_async_copy(result_tiles.at[t], out.at[:, pl.ds(t * tile, tile)], out_sem.at[t])
+
     def part_copy(t):
         return remote(partial.at[t], incoming.at[t], part_send.at[t], part_recv.at[t], at_dp(sibling))
 
@@ -535,7 +561,7 @@
     for t in range(tiles):
         cols = slice(t * tile, (t + 1) * tile)
         pruned = weight[:, cols].astype(jnp.float32) - full[own_rows, cols].astype(jnp.float32)
-        out[:, cols] = product(core, cols) * (1.0 / math.sqrt(tokens)) + decay_rate * pruned
+        result_tiles[t] = product(core, cols) * (1.0 / math.sqrt(tokens)) + decay_rate * pruned
 
     for k in range(1, chips):
         flip_copy(k, peer_chip(k)).wait_recv()
@@ -549,7 +575,8 @@
     for t in range(tiles):
         cols = slice(t * tile, (t + 1) * tile)
         part_copy(t).wait_recv()
-        out[:, cols] = out[:, cols] + incoming[t].astype(jnp.float32) * (1.0 / math.sqrt(tokens))
+        result_tiles[t] = result_tiles[t] + incoming[t].astype(jnp.float32) * (1.0 / math.sqrt(tokens))
+        out_copy(t).start()
     pair_copy.wait_recv()
     flips[...] = counts[chips] + counts[chips + 1]
 
@@ -585,6 +612,8 @@
         return carry
 
     lax.fori_loop(0, steps, drain, 0)
+    for t in range(tiles):
+        out_copy(t).wait()
 
 
 def fused_body(activations, cotangent, weight, norm_gain, pair_mask, earlier_mask):
@@ -609,7 +638,7 @@
             jax.ShapeDtypeStruct((8, 128), jnp.int32),
         ),
         in_specs=[hbm, hbm, vmem, vmem, hbm, vmem],
-        out_specs=(vmem, vmem),
+        out_specs=(hbm, vmem),
         scratch_shapes=[
             pltpu.VMEM((replicas, 2 * groups, width), bf),
             pltpu.VMEM((width, width), bf),
@@ -628,6 +657,9 @@
             pltpu.VMEM((width // 4, width), jnp.int32),
             pltpu.VMEM((groups, width), jnp.int32),
             dma((2,)), dma((micro,)),
+            pltpu.VMEM((width, width), bf),
+            pltpu.VMEM((tiles, shard_rows, tile), f32),
+            dma((tiles,)),
             dma((3, 2)), dma((chips, 2)), dma((chips,)), dma((chips,)),
             dma((steps,)), dma((steps,)), dma((steps,)), dma((steps,)),
             dma((chips, steps)), dma((chips, steps)), dma((6, steps)), dma((2 * chips, steps)),

time: 124 us -> 124 us (level)
  no operation moved by 1% of the time
where the time goes in v3:
time: 124 us
  Pallas kernels  119 us (96%)
  local copies, waits for them, and re-layouts  3.13 us (3%)
  other arithmetic  1.32 us (1%)
    pallas_call x1, Pallas kernels, fused_body(): pl.pallas_call(functools.partial(fused_kernel, chunk, rows * replicas), o...  119 us
    unnamed x1, local copies, waits for them, and re-layouts  3.13 us

profile of v3, /device:TPU:0, one launch (start us, length us, event | category | flops | bytes accessed | tf_op | source)
XLA Modules:
  0.0 123.8 jit_solution(11094188720537340761)
XLA Ops:
  0.6 118.7 %fused_step.1 = (f32[256,2048]{1,0:T(8,128)}, s32[8,128]{1,0:T(8,128)}) custom-call(bf16[4,64,2048]{2,1,0:T(8,128)(2,1)} %act.1, bf16[4,64,2048]{2,1,0:T(8,128)(2,1)} %cot.1, bf16[256,2048]{1,0:T(8,128)(2,1)} %bitcast.7, f32[1,2048]{1,0:T(1,128)} %gain.1, s32[512,2048]{1,0:T(8,128)} %bitcast.5, s32[64,2048]{1,0:T(8,128)} %bitcast.8), custom_call_target="tpu_custom_call" | custom-call | tf_op jit(solution)/shard_map/fused_step/pallas_call | solution.py:634
  119.3 1.3 %reduce_sum.9 = s32[]{:T(128)} reduce(s32[8,128]{1,0:T(8,128)} %get-tuple-element.5, s32[]{:T(128)} %constant.0.clone.1), dimensions={0,1}, to_apply=%region_0.0 | reduce | flops 1023 | bytes 4104 | tf_op jit(solution)/shard_map/reduce_sum | solution.py:675
  120.7 3.1 %copy.9 = f32[1,256,2048]{2,1,0:T(8,128)} copy(f32[1,256,2048]{2,1,0:T(8,128)} %bitcast.6) | data formatting | bytes 4194304
